TPU v7x, 256 devices: a whole 4x4x8 slice. The times are simulated.
256 devices in a mesh: dp: 32 (over z_lo, x, y), mp: 8 (over z_hi, core).
Axes of the slice: x: 4, y: 4, z: 8 (z_hi: 4, z_lo: 2; z = z_hi * 2 + z_lo), core: 2. Of those that a mesh axis runs over, the one named last changes fastest.
Arguments:
- hidden_states: bfloat16 [16384, 4096], P('dp', 'mp'), may hold values from -40 to 40
- norm_gain: float32 [1, 4096], replicated, may hold values from 0.1 to 1.9
- query_weight: bfloat16 [1, 4096, 4096], P(None, 'dp', 'mp'), may hold values from -0.01171875 to 0.01171875
- keyvalue_weight: bfloat16 [1, 4096, 2, 4096], P(None, 'dp', None, 'mp'), may hold values from -0.09375 to 0.09375
- output_weight: bfloat16 [1, 4096, 4096], P(None, 'dp', 'mp'), may hold values from -0.09375 to 0.09375
- position_bias: float32 [1, 32, 64], P(None, None, 'mp'), may hold values from -8 to 250
- lengths: int32 [128], P('dp'), may hold values from 16 to 128
Outputs:
- layer_output: bfloat16 [16384, 4096], P('dp', 'mp')
All inputs are finite; a program needn't handle non-finite values.
Results may differ from a plain program's by a relative error of at most 0.006.
Values may be sent and summed in bfloat16 or wider, within the bound.
A program may use at most 128 MiB of HBM per device.

v0:
```python
import jax
import jax.numpy as jnp
import numpy as np
from jax import lax
from jax.sharding import PartitionSpec as P

DH = 64
BUCKETS = 32
DIST = 128
LEN = 128
epsilon = 1e-06


def side_by_side(arrays, axis, dim, along):
    columns = [a.reshape(*a.shape[:along], -1) for a in arrays]
    both = jnp.concatenate(columns, axis=along)
    filled, at, outs = (lax.all_gather(both, axis, axis=dim, tiled=True), 0, [])
    for a, column in zip(arrays, columns):
        piece = filled[..., at : at + column.shape[along]]
        outs.append(piece.reshape(*piece.shape[:along], *a.shape[along:]))
        at += column.shape[along]
    return tuple(outs)


def bucket_table():
    half_count = BUCKETS // 2
    exact_count = half_count // 2
    positions = np.arange(LEN)
    relative = positions[None, :] - positions[:, None]
    distance = np.abs(relative)
    scaled = (
        np.log(np.maximum(distance, 1) / exact_count)
        / np.log(DIST / exact_count)
        * (half_count - exact_count)
    )
    far_bucket = np.minimum(exact_count + np.floor(scaled + 1e-09).astype(np.int32), half_count - 1)
    near_bucket = np.where(distance < exact_count, distance, far_bucket)
    return (near_bucket + np.where(relative > 0, half_count, 0)).astype(np.int32)


def normed_rows(hidden, gain_row):
    values = hidden.astype(jnp.float32)
    mean_square = jnp.mean(values * values, axis=-1, keepdims=True)
    return (values * lax.rsqrt(mean_square + epsilon) * gain_row).astype(jnp.bfloat16)


def add_projections(query_acc, pair_acc, normed, query_piece, pair_piece):
    query_acc = jnp.dot(normed, query_piece, preferred_element_type=jnp.float32)
    pair_acc = jnp.einsum("td,dcf->ctf", normed, pair_piece, preferred_element_type=jnp.float32)
    return (query_acc, pair_acc)


def local(
    hidden_states, norm_gain, query_weight, keyvalue_weight, output_weight, position_bias, lengths
):
    captions = lengths.shape[0]
    tokens_here = hidden_states.shape[0]
    heads_here = position_bias.shape[2]
    inner_here = heads_here * DH
    bucket_onehot = jnp.asarray(
        (bucket_table()[:, :, None] == np.arange(BUCKETS)[None, None, :]).astype(np.float32)
    )
    visible = jnp.arange(LEN)[None, :] < lengths[:, None]
    hidden = hidden_states
    gathered = lax.all_gather(hidden, "mp", axis=1, tiled=True)
    normed = normed_rows(gathered, norm_gain[0])
    zero_queries = jnp.zeros((tokens_here, inner_here), jnp.float32)
    zero_pairs = jnp.zeros((2, tokens_here, inner_here), jnp.float32)
    query_rows = query_weight[0]
    pair_rows = keyvalue_weight[0]
    out_rows = output_weight[0]
    shard_rows = side_by_side((query_rows, pair_rows, out_rows), "dp", 0, 1)
    query_acc, pair_acc = add_projections(
        zero_queries, zero_pairs, normed, shard_rows[0], shard_rows[1]
    )
    whole_rows = shard_rows[2]
    query_acc, pair_acc, out_full = (query_acc, pair_acc, whole_rows)
    queries = query_acc.astype(jnp.bfloat16).reshape(captions, LEN, heads_here, DH)
    key_rows = pair_acc[0].astype(jnp.bfloat16).reshape(captions, LEN, heads_here, DH)
    value_rows = pair_acc[1].astype(jnp.bfloat16).reshape(captions, LEN, heads_here, DH)
    position_terms = jnp.einsum(
        "qkb,bh->hqk", bucket_onehot, position_bias[0], precision=lax.Precision.HIGHEST
    )
    scores = (
        jnp.einsum("cqhe,ckhe->chqk", queries, key_rows, preferred_element_type=jnp.float32)
        + position_terms[None]
    )
    scores = jnp.where(visible[:, None, None, :], scores, -1e30)
    maxima = jnp.max(scores, axis=-1, keepdims=True)
    raised = jnp.exp(scores - maxima)
    weights = (raised / jnp.sum(raised, axis=-1, keepdims=True)).astype(jnp.bfloat16)
    mixture = jnp.einsum("chqk,ckhe->cqhe", weights, value_rows, preferred_element_type=jnp.float32)
    attended = mixture.astype(jnp.bfloat16).reshape(tokens_here, inner_here)
    partial_out = jnp.einsum("tf,df->td", attended, out_full, preferred_element_type=jnp.float32)
    reduced = lax.psum_scatter(
        partial_out.astype(jnp.bfloat16), "mp", scatter_dimension=1, tiled=True
    ).astype(jnp.float32)
    hidden = (hidden.astype(jnp.float32) + reduced).astype(jnp.bfloat16)
    return hidden


def solution(mesh):
    in_specs = (
        P("dp", "mp"),
        P(),
        P(None, "dp", "mp"),
        P(None, "dp", None, "mp"),
        P(None, "dp", "mp"),
        P(None, None, "mp"),
        P("dp"),
    )
    out_specs = P("dp", "mp")
    return jax.shard_map(local, mesh=mesh, in_specs=in_specs, out_specs=out_specs, check_vma=False)
```

profile of v0, /device:TPU:65, one launch (start us, length us, event | category | flops | bytes accessed | tf_op | source)
XLA Modules:
  0.0 413.0 jit_solution(2870992319001672972)
XLA Ops:
  6.5 0.7 all-gather.5.cloned.1.call-update
  7.3 1.2 copy.28
  8.5 1.0 copy.17
  9.5 1.0 copy.19
  10.5 0.8 pad_maximum_fusion
  11.4 1.2 convolution_bitcast_fusion
  12.7 0.2 copy.23
  12.9 0.1 iota_compare_fusion
  13.0 51.6 %all-gather.5.cloned.1.call-done = bf16[512,4096]{1,0:T(8,128)(2,1)} async-done(((bf16[512,512]{1,0:T(8,128)(2,1)}), bf16[512,4096]{1,0:T(8,128)(2,1)}) %all-gather.5.cloned.1.call-update) | async-done | bytes 4194320 | tf_op jit(solution)/shard_map/all_gather | solution.py:65
  64.6 3.1 fusion.1
  67.7 222.8 %all-gather.3.cloned.1.call-done = bf16[4096,2048]{0,1:T(8,128)(2,1)} async-done(((bf16[128,2048]{0,1:T(8,128)(2,1)}), bf16[4096,2048]{0,1:T(8,128)(2,1)}) %all-gather.3.cloned.1.call-update) | async-done | bytes 16777232 | tf_op jit(solution)/shard_map/all_gather | solution.py:17
  290.5 7.9 %slice.22 = bf16[4096,1024]{0,1:T(8,128)(2,1)} slice(bf16[4096,2048]{0,1:T(8,128)(2,1)} %all-gather.3.cloned.1.call-done), slice={[0:4096], [512:1536]} | slice | bytes 16777216 | tf_op jit(solution)/shard_map/slice | solution.py:19
  298.4 7.3 %fusion.13 = bf16[2,512,512]{1,2,0:T(8,128)(2,1)S(1)} fusion(bf16[4096,2,512]{0,2,1:T(8,128)(2,1)} %bitcast.35, bf16[512,4096]{1,0:T(8,128)(2,1)S(1)} %copy-done.1, f32[4096]{0:T(1024)S(1)} %bitcast.40, f32[512]{0:T(512)S(1)} %add_rsqrt_fusion), kind=kOutput, calls=%fused_computation.17 | convolution fusion | flops 4303880192 | bytes 13649920 | tf_op jit(solution)/shard_map/td,dcf->ctf/dot_general | solution.py:49
  305.7 0.1 fusion.45
  305.8 0.1 convert_element_type.45
  305.9 5.8 %fusion.16 = bf16[512,512]{1,0:T(8,128)(2,1)S(1)} fusion(bf16[4096,2048]{0,1:T(8,128)(2,1)} %all-gather.3.cloned.1.call-done, bf16[512,4096]{1,0:T(8,128)(2,1)} %all-gather.5.cloned.1.call-done, f32[4096]{0:T(1024)S(1)} %bitcast.41, f32[512]{0:T(512)S(1)} %add_rsqrt_fusion), kind=kOutput, calls=%fused_computation.18 | convolution fusion | flops 2156134400 | bytes 8931328 | tf_op jit(solution)/shard_map/dot_general | solution.py:48
  311.7 0.5 reshape.48
  312.3 0.1 convert_element_type.43
  312.4 2.5 fusion.46
  315.0 2.0 fusion.19
  317.0 0.4 copy.26
  317.4 6.5 %convolution_convert_fusion = bf16[512,4096]{1,0:T(8,128)(2,1)} fusion(bf16[4096,2048]{0,1:T(8,128)(2,1)} %all-gather.3.cloned.1.call-done, bf16[64,8,4,128]{3,2,1,0:T(4,128)(2,1)S(1)} %bitcast.36), kind=kOutput, calls=%fused_computation.6 | convolution fusion | flops 2149580800 | bytes 8912896 | tf_op jit(solution)/shard_map/tf,df->td/dot_general | solution.py:94
  323.9 80.5 %reduce-scatter.2.cloned.1.call-done = bf16[512,512]{1,0:T(8,128)(2,1)} async-done(((bf16[512,4096]{1,0:T(8,128)(2,1)}), bf16[512,512]{1,0:T(8,128)(2,1)}) %reduce-scatter.2.cloned.1.call-update) | async-done | bytes 524304 | tf_op jit(solution)/shard_map/reduce_scatter | solution.py:95
  404.4 2.0 add_convert_fusion
  (18 shorter events, 0.1 us)
Async XLA Ops:
  6.5 4.9 %copy-start = (f32[1,32,8]{1,2,0:T(8,128)S(1)}, f32[1,32,8]{1,2,0:T(8,128)}, u32[]{:S(2)}) copy-start(f32[1,32,8]{1,2,0:T(8,128)} %param.13) | copy-start | bytes 3076
  6.5 4.9 %copy-start.2 = (f32[128,128,32]{1,2,0:T(8,128)S(1)}, f32[128,128,32]{1,2,0:T(8,128)}, u32[]{:S(2)}) copy-start(f32[128,128,32]{1,2,0:T(8,128)} %constant.13.clone) | copy-start | bytes 6291460
  6.5 6.4 %copy-start.5 = (s32[4]{0:T(128)S(1)}, s32[4]{0:T(128)}, u32[]{:S(2)}) copy-start(s32[4]{0:T(128)} %param.14) | copy-start | bytes 52
  6.5 58.0 %all-gather.5.cloned.1.call-start = ((), (), s32[]{:S(2)}) async-start(), calls=%async_computation.2 | async-start | bytes 4718592 | tf_op jit(solution)/shard_map/all_gather | solution.py:65
  7.3 283.2 %all-gather.3.cloned.1.call-start = ((), (), s32[]{:S(2)}) async-start(), calls=%async_computation.1 | async-start | bytes 17301504 | tf_op jit(solution)/shard_map/all_gather | solution.py:17
  11.4 393.1 %reduce-scatter.2.cloned.1.call-start = ((), (), s32[]{:S(2)}) async-start(), calls=%async_computation.3 | async-start | bytes 4718592 | tf_op jit(solution)/shard_map/reduce_scatter | solution.py:95
  67.6 230.7 %copy-start.4 = (f32[1,4096]{1,0:T(1,128)S(1)}, f32[1,4096]{1,0:T(1,128)}, u32[]{:S(2)}) copy-start(f32[1,4096]{1,0:T(1,128)} %param.9) | copy-start | bytes 49156
  290.5 7.9 %copy-start.1 = (bf16[512,4096]{1,0:T(8,128)(2,1)S(1)}, bf16[512,4096]{1,0:T(8,128)(2,1)}, u32[]{:S(2)}) copy-start(bf16[512,4096]{1,0:T(8,128)(2,1)} %all-gather.5.cloned.1.call-done) | copy-start | bytes 12582916
  323.9 80.5 %copy-start.3 = (bf16[512,512]{1,0:T(8,128)(2,1)S(1)}, bf16[512,512]{1,0:T(8,128)(2,1)}, u32[]{:S(2)}) copy-start(bf16[512,512]{1,0:T(8,128)(2,1)} %param.8) | copy-start | bytes 1572868
Sparse Core Ops, SparseCore 0:
  9.2 55.3 all-gather.4
  66.3 224.1 all-gather.2
  324.1 80.3 reduce-scatter.1
where the time goes:
time: 413 us
  waiting for transfers between devices  356 us (86%)
  matrix products  25.4 us (6%)
  between operations  13.2 us (3%)
  local copies, waits for them, and re-layouts  12.6 us (3%)
  other arithmetic  6 us (1%)
    all_gather x1, waiting for transfers between devices, side_by_side(): filled, at, outs = (lax.all_gather(both, axis, axis=dim, tiled=True), 0, [])  223 us
    reduce_scatter x1, waiting for transfers between devices, local(): lax.psum_scatter(partial_out.astype(jnp.bfloat16), 'mp', scatter_dimensio...  80.5 us
    all_gather x1, waiting for transfers between devices, local(): gathered = lax.all_gather(hidden, 'mp', axis=1, tiled=True)  51.6 us
  transfers between devices with their start and end apart: 3, of which 3 were waited for; matrix products, arithmetic and copies ran while one was open for 2% of the time, Pallas kernels for 0%

commit v1 on v0

--- a/solution.py
+++ b/solution.py
@@ -62,7 +62,13 @@
     )
     visible = jnp.arange(LEN)[None, :] < lengths[:, None]
     hidden = hidden_states
-    gathered = lax.all_gather(hidden, "mp", axis=1, tiled=True)
+    upper = lax.all_to_all(
+        jnp.stack([hidden for _ in range(lax.axis_size("mp"))], 0),
+        axis_name="mp",
+        split_axis=0,
+        concat_axis=0,
+    )
+    gathered = jnp.concatenate(upper, 1)
     normed = normed_rows(gathered, norm_gain[0])
     zero_queries = jnp.zeros((tokens_here, inner_here), jnp.float32)
     zero_pairs = jnp.zeros((2, tokens_here, inner_here), jnp.float32)

time: 413 us -> 436 us (1.056)
  local copies, waits for them, and re-layouts: 12.6 us -> 23.1 us
  starting transfers between devices: 0.08 us -> 8.53 us
  other arithmetic: 6 us -> 11.8 us
    all_to_all x0 -> x1, waiting for transfers between devices: none -> 128 us  [local(): lax.all_to_all(jnp.stack([hidden for _ in range(lax.axis_size('mp'))], 0)...]
    all_gather x1, waiting for transfers between devices: 223 us -> 149 us  [side_by_side(): filled, at, outs = (lax.all_gather(both, axis, axis=dim, tiled=True), 0, [])]
    all_gather x1 -> x0, waiting for transfers between devices: 51.6 us -> none  [local(): gathered = lax.all_gather(hidden, 'mp', axis=1, tiled=True)]
    all_to_all x0 -> x1, starting transfers between devices: none -> 8.53 us  [local(): lax.all_to_all(jnp.stack([hidden for _ in range(lax.axis_size('mp'))], 0)...]
    all_to_all x0 -> x1, local copies, waits for them, and re-layouts: none -> 6.5 us  [local(): lax.all_to_all(jnp.stack([hidden for _ in range(lax.axis_size('mp'))], 0)...]
    reduce_scatter x1, waiting for transfers between devices: 80.5 us -> 75.3 us  [local(): lax.psum_scatter(partial_out.astype(jnp.bfloat16), 'mp', scatter_dimensio...]
  transfers between devices with their start and end apart: 3 -> 3, of which waited for: 3 -> 3; matrix products, arithmetic and copies ran while one was open for 2% -> 5% of each run, Pallas kernels for 0% -> 0%
where the time goes in v1:
time: 436 us; the launch traced here: 435 us
  waiting for transfers between devices  353 us (81%)
  matrix products  25.4 us (6%)
  local copies, waits for them, and re-layouts  23.1 us (5%)
  between operations  13.5 us (3%)
  other arithmetic  11.8 us (3%)
  starting transfers between devices  8.53 us (2%)
    all_gather x1, waiting for transfers between devices, side_by_side(): filled, at, outs = (lax.all_gather(both, axis, axis=dim, tiled=True), 0, [])  149 us
    all_to_all x1, waiting for transfers between devices, local(): lax.all_to_all(jnp.stack([hidden for _ in range(lax.axis_size('mp'))], 0)...  128 us
    reduce_scatter x1, waiting for transfers between devices, local(): lax.psum_scatter(partial_out.astype(jnp.bfloat16), 'mp', scatter_dimensio...  75.3 us
  transfers between devices with their start and end apart: 3, of which 3 were waited for; matrix products, arithmetic and copies ran while one was open for 5% of the time, Pallas kernels for 0%

profile of v1, /device:TPU:65, one launch (start us, length us, event | category | flops | bytes accessed | tf_op | source)
XLA Modules:
  0.0 435.0 jit_solution(18194182420709615815)
XLA Ops:
  6.5 1.0 copy.37
  7.6 1.0 copy.39
  8.6 1.2 copy.51
  9.8 0.8 pad_maximum_fusion
  10.6 3.4 stack.2
  14.0 8.5 %all-to-all-start = ((bf16[8,512,512]{2,1,0:T(8,128)(2,1)}), bf16[8,512,512]{2,1,0:T(8,128)(2,1)}, u32[]{:S(2)}, u32[]{:S(2)}) async-start(bf16[8,512,512]{2,1,0:T(8,128)(2,1)} %stack.2), calls=%async_computation | async-start | bytes 8388608 | tf_op jit(solution)/shard_map/all_to_all | solution.py:65
  22.5 0.5 broadcast.36
  23.1 0.6 reduce.5
  23.7 1.2 convolution_bitcast_fusion
  25.2 127.9 %all-to-all-done = bf16[8,512,512]{2,1,0:T(8,128)(2,1)} async-done(((bf16[8,512,512]{2,1,0:T(8,128)(2,1)}), bf16[8,512,512]{2,1,0:T(8,128)(2,1)}, u32[]{:S(2)}, u32[]{:S(2)}) %all-to-all-start) | async-done | bytes 4194336 | tf_op jit(solution)/shard_map/all_to_all | solution.py:65
  153.1 6.5 %copy.40 = bf16[8,512,512]{1,2,0:T(8,128)(2,1)} copy(bf16[8,512,512]{2,1,0:T(8,128)(2,1)} %all-to-all-done) | data formatting | bytes 8388608 | tf_op jit(solution)/shard_map/all_to_all | solution.py:65
  159.6 3.3 multiply_reduce_fusion
  163.1 2.6 multiply_convert_fusion
  165.6 2.5 fusion.2
  168.1 149.4 %all-gather.2.cloned.1.call-done = bf16[4096,2048]{0,1:T(8,128)(2,1)} async-done(((bf16[128,2048]{0,1:T(8,128)(2,1)}), bf16[4096,2048]{0,1:T(8,128)(2,1)}) %all-gather.2.cloned.1.call-update) | async-done | bytes 16777232 | tf_op jit(solution)/shard_map/all_gather | solution.py:17
  317.5 5.8 %fusion.8 = bf16[512,512]{1,0:T(8,128)(2,1)S(1)} fusion(bf16[512,4096]{0,1:T(8,128)(2,1)} %fusion.2, bf16[4096,2048]{0,1:T(8,128)(2,1)} %all-gather.2.cloned.1.call-done), kind=kOutput, calls=%fused_computation.16 | convolution fusion | flops 2147745792 | bytes 8912896 | tf_op jit(solution)/shard_map/dot_general | solution.py:48
  323.4 0.5 reshape.66
  323.9 7.9 %slice.22 = bf16[4096,1024]{0,1:T(8,128)(2,1)} slice(bf16[4096,2048]{0,1:T(8,128)(2,1)} %all-gather.2.cloned.1.call-done), slice={[0:4096], [512:1536]} | slice | bytes 16777216 | tf_op jit(solution)/shard_map/slice | solution.py:19
  331.8 7.3 %fusion.7 = bf16[2,512,512]{1,2,0:T(8,128)(2,1)S(1)} fusion(bf16[4096,2,512]{0,2,1:T(8,128)(2,1)} %bitcast.43, bf16[512,4096,1]{0,1,2:T(8,128)(2,1)S(1)} %bitcast.44), kind=kOutput, calls=%fused_computation.15 | convolution fusion | flops 4295491584 | bytes 13631488 | tf_op jit(solution)/shard_map/td,dcf->ctf/dot_general | solution.py:49
  339.4 2.5 fusion.36
  341.9 2.0 fusion.11
  344.4 6.5 %convolution_convert_fusion = bf16[512,4096]{1,0:T(8,128)(2,1)} fusion(bf16[4096,2048]{0,1:T(8,128)(2,1)} %all-gather.2.cloned.1.call-done, bf16[64,8,4,128]{3,2,1,0:T(4,128)(2,1)S(1)} %bitcast.45), kind=kOutput, calls=%fused_computation.6 | convolution fusion | flops 2149580800 | bytes 8912896 | tf_op jit(solution)/shard_map/tf,df->td/dot_general | solution.py:100
  350.9 75.3 %reduce-scatter.2.cloned.1.call-done = bf16[512,512]{1,0:T(8,128)(2,1)} async-done(((bf16[512,4096]{1,0:T(8,128)(2,1)}), bf16[512,512]{1,0:T(8,128)(2,1)}) %reduce-scatter.2.cloned.1.call-update) | async-done | bytes 524304 | tf_op jit(solution)/shard_map/reduce_scatter | solution.py:101
  426.2 2.0 add_convert_fusion
  (26 shorter events, 1.3 us)
Async XLA Ops:
  6.5 17.1 %copy-start = (f32[1,32,8]{1,2,0:T(8,128)S(1)}, f32[1,32,8]{1,2,0:T(8,128)}, u32[]{:S(2)}) copy-start(f32[1,32,8]{1,2,0:T(8,128)} %param.13) | copy-start | bytes 3076
  6.5 311.0 %all-gather.2.cloned.1.call-start = ((), (), s32[]{:S(2)}) async-start(), calls=%async_computation.2 | async-start | bytes 17301504 | tf_op jit(solution)/shard_map/all_gather | solution.py:17
  14.0 9.1 %copy-start.5 = (f32[1,4096]{1,0:T(1,128)S(1)}, f32[1,4096]{1,0:T(1,128)}, u32[]{:S(2)}) copy-start(f32[1,4096]{1,0:T(1,128)} %param.9) | copy-start | bytes 49156
  14.0 9.7 %copy-start.4 = (f32[128,128,32]{1,2,0:T(8,128)S(1)}, f32[128,128,32]{1,2,0:T(8,128)}, u32[]{:S(2)}) copy-start(f32[128,128,32]{1,2,0:T(8,128)} %constant.13.clone) | copy-start | bytes 6291460
  14.0 11.2 %copy-start.6 = (s32[4]{0:T(128)S(1)}, s32[4]{0:T(128)}, u32[]{:S(2)}) copy-start(s32[4]{0:T(128)} %param.14) | copy-start | bytes 52
  14.0 139.1 %all-to-all-start = ((bf16[8,512,512]{2,1,0:T(8,128)(2,1)}), bf16[8,512,512]{2,1,0:T(8,128)(2,1)}, u32[]{:S(2)}, u32[]{:S(2)}) async-start(bf16[8,512,512]{2,1,0:T(8,128)(2,1)} %stack.2), calls=%async_computation | async-start | bytes 8388608 | tf_op jit(solution)/shard_map/all_to_all | solution.py:65
  22.5 403.7 %reduce-scatter.2.cloned.1.call-start = ((), (), s32[]{:S(2)}) async-start(), calls=%async_computation.3 | async-start | bytes 4718592 | tf_op jit(solution)/shard_map/reduce_scatter | solution.py:101
  159.6 3.4 copy-start.1
  323.9 7.9 %copy-start.2 = (bf16[8,512,512]{1,2,0:T(8,128)(2,1)S(1)}, bf16[8,512,512]{1,2,0:T(8,128)(2,1)}, u32[]{:S(2)}) copy-start(bf16[8,512,512]{1,2,0:T(8,128)(2,1)} %multiply_convert_fusion) | copy-start | bytes 12582916
  350.9 75.3 %copy-start.3 = (bf16[512,512]{1,0:T(8,128)(2,1)S(1)}, bf16[512,512]{1,0:T(8,128)(2,1)}, u32[]{:S(2)}) copy-start(bf16[512,512]{1,0:T(8,128)(2,1)} %param.8) | copy-start | bytes 1572868
Sparse Core Ops, SparseCore 0:
  10.7 306.7 all-gather.1
  351.0 75.1 reduce-scatter.1
